TPU v7x, 32 devices: a whole 2x2x4 slice. The times are simulated.
32 devices in a mesh: row: 4 (over z), col: 4 (over y, core), rep: 2 (over x).
Axes of the slice: x: 2, y: 2, z: 4, core: 2. Of those that a mesh axis runs over, the one named last changes fastest.
Arguments:
- upstream: float32 [16384, 16384], P('row', ('col', 'rep')), may hold values from -0.046875 to 0.046875
- input_panel: float32 [16384, 1024], P('row', ('col', 'rep')), may hold values from -6 to 6
Outputs:
- panel_grad: float32 [16384, 1024], P('row', ('col', 'rep'))
All inputs are finite; a program needn't handle non-finite values.
Results may differ from a plain program's by a relative error of at most 0.000071.
Values sent between devices are 32-bit elements; how exact they have to be, the bound alone decides.
A program may use at most 192 MiB of HBM per device.

v0:
```python
import jax
import jax.numpy as jnp
from jax import lax
from jax.sharding import PartitionSpec as P


def from_root(x, axis, root):
    mine = lax.axis_index(axis) == root
    return lax.psum(jnp.where(mine, x, jnp.zeros_like(x)), axis)


def row_total(buffer):
    return lax.psum_scatter(buffer, "row", scatter_dimension=0, tiled=True)


def per_device(upstream, input_panel):
    precise = lax.Precision.HIGHEST
    row_count, col_count = upstream.shape
    row_index = lax.axis_index("row")
    col_index = lax.axis_index(("col", "rep"))
    rows_global = row_index * row_count + lax.broadcasted_iota(jnp.int32, (row_count, col_count), 0)
    cols_global = col_index * col_count + lax.broadcasted_iota(jnp.int32, (row_count, col_count), 1)
    lower_tile = jnp.where(cols_global <= rows_global, upstream, jnp.float32(0.0))
    row_band = lax.all_gather(input_panel, ("col", "rep"), axis=1, tiled=True)
    upper_part = lax.dot_general(
        lower_tile,
        row_band,
        (((0,), (0,)), ((), ())),
        precision=precise,
        preferred_element_type=jnp.float32,
    )
    source_row = col_index * col_count // row_count
    offset = col_index * col_count - source_row * row_count
    column_rows = from_root(
        lax.dynamic_slice_in_dim(row_band, offset, col_count, 0), "row", source_row
    )
    buffer = lax.all_to_all(upper_part, ("col", "rep"), split_axis=1, concat_axis=0, tiled=True)
    lower_total = lax.psum_scatter(
        lax.dot_general(
            column_rows,
            lower_tile,
            (((0,), (1,)), ((), ())),
            precision=precise,
            preferred_element_type=jnp.float32,
        ),
        ("col", "rep"),
        scatter_dimension=0,
        tiled=True,
    )
    return row_total(buffer) + jnp.transpose(lower_total)


def solution(mesh):
    placed = (P("row", ("col", "rep")), P("row", ("col", "rep")))
    return jax.shard_map(
        per_device, mesh=mesh, in_specs=placed, out_specs=P("row", ("col", "rep")), check_vma=False
    )
```

profile of v0, /device:TPU:0, one launch (start us, length us, event | category | flops | bytes accessed | tf_op | source)
XLA Modules:
  0.0 751.1 jit_solution(11321924936020843688)
XLA Ops:
  6.5 0.0 all-gather.2.cloned.1.call-start
  6.5 0.7 all-gather.2.cloned.1.call-update
  7.3 0.0 all-reduce.2.cloned.1.call-start
  7.4 23.6 %compare_select_fusion.7 = f32[4096,2048]{1,0:T(8,128)} fusion(f32[4096,2048]{1,0:T(8,128)} %param.2, s32[2048]{0:T(1024)S(1)} %iota_add_fusion.1, s32[4096]{0:T(1024)S(1)} %iota_add_fusion), kind=kLoop, calls=%fused_computation.clone.1.clone.1 | loop fusion | flops 16777216 | bytes 67133440 | tf_op jit(solution)/shard_map/dot_general | solution.py:25
  30.9 74.0 %all-gather.2.cloned.1.call-done = f32[4096,1024]{1,0:T(8,128)} async-done(((f32[4096,128]{1,0:T(8,128)}), f32[4096,1024]{1,0:T(8,128)}) %all-gather.2.cloned.1.call-update) | async-done | bytes 16777232 | tf_op jit(solution)/shard_map/all_gather | solution.py:24
  105.0 8.5 %dynamic-slice_select_fusion = f32[2048,1024]{1,0:T(8,128)} fusion(f32[4096,1024]{1,0:T(8,128)} %all-gather.2.cloned.1.call-done, s32[]{:T(128)S(6)} %select_n.23, pred[]{:T(512)S(6)} %eq.3), kind=kLoop, calls=%fused_computation.9 | loop fusion | flops 2097152 | bytes 16777220 | tf_op jit(solution)/shard_map/jit(_where)/select_n | solution.py:9
  113.5 0.0 all-reduce.2.cloned.1.call-update
  113.5 0.0 reduce-scatter.3.cloned.1.call-start
  113.6 124.2 %fusion.1 = f32[2048,1024]{0,1:T(8,128)S(1)} fusion(f32[4096,1024]{1,0:T(8,128)} %all-gather.2.cloned.1.call-done, f32[4096,2048]{1,0:T(8,128)} %compare_select_fusion.7), kind=kOutput, calls=%fused_computation.2 | convolution fusion | flops 103079215104 | bytes 58720256 | tf_op jit(solution)/shard_map/dot_general | solution.py:25
  237.7 96.0 %all_to_all.19 = f32[2048,8,128]{0,2,1:T(8,128)S(1)} all-to-all(f32[2048,8,128]{0,2,1:T(8,128)S(1)} %bitcast.13), channel_id=1, replica_groups=mesh['row'=4,'col'=4,'rep'=2] {'col','rep'}, dimensions={1} | all-to-all | bytes 16777216 | tf_op jit(solution)/shard_map/all_to_all | solution.py:37
  333.7 3.8 copy.5
  337.5 0.0 reduce-scatter.3.cloned.1.call-update
  337.5 0.0 reduce-scatter.5.cloned.1.call-start
  337.6 66.9 %all-reduce.2.cloned.1.call-done = f32[2048,1024]{1,0:T(8,128)} async-done(((f32[2048,1024]{1,0:T(8,128)}), f32[2048,1024]{1,0:T(8,128)}) %all-reduce.2.cloned.1.call-update) | async-done | bytes 8388624 | tf_op jit(solution)/shard_map/psum | solution.py:9
  404.5 220.5 %fusion = f32[1024,4096]{1,0:T(8,128)} fusion(f32[2048,1024]{1,0:T(8,128)} %all-reduce.2.cloned.1.call-done, f32[4096,2048]{1,0:T(8,128)} %param.2, s32[2048]{0:T(1024)S(1)} %iota_add_fusion.1, s32[4096]{0:T(1024)S(1)} %iota_add_fusion), kind=kOutput, calls=%fused_computation.1 | convolution fusion | flops 103095992320 | bytes 58744832 | tf_op jit(solution)/shard_map/dot_general | solution.py:39
  625.0 0.0 reduce-scatter.5.cloned.1.call-update
  625.0 0.0 reduce-scatter.3.cloned.1.call-done
  625.1 115.3 %reduce-scatter.5.cloned.1.call-done = f32[128,4096]{1,0:T(8,128)} async-done(((f32[1024,4096]{1,0:T(8,128)}), f32[128,4096]{1,0:T(8,128)}) %reduce-scatter.5.cloned.1.call-update) | async-done | bytes 2097168 | tf_op jit(solution)/shard_map/reduce_scatter | solution.py:38
  740.3 2.4 bitcast_add_fusion
  742.8 1.8 copy.4
  (2 shorter events, 0.0 us)
Async XLA Ops:
  6.5 98.5 %all-gather.2.cloned.1.call-start = ((), (), s32[]{:S(2)}) async-start(), calls=%async_computation.3 | async-start | bytes 18874368 | tf_op jit(solution)/shard_map/all_gather | solution.py:24
  7.3 397.2 %all-reduce.2.cloned.1.call-start = ((), (), s32[]{:S(2)}) async-start(), calls=%async_computation.5 | async-start | bytes 16777216 | tf_op jit(solution)/shard_map/psum | solution.py:9
  113.5 511.6 %reduce-scatter.3.cloned.1.call-start = ((), (), s32[]{:S(2)}) async-start(), calls=%async_computation.4 | async-start | bytes 10485760 | tf_op jit(solution)/shard_map/reduce_scatter | solution.py:13
  337.5 402.8 %reduce-scatter.5.cloned.1.call-start = ((), (), s32[]{:S(2)}) async-start(), calls=%async_computation.6 | async-start | bytes 18874368 | tf_op jit(solution)/shard_map/reduce_scatter | solution.py:38
Sparse Core Ops, SparseCore 0:
  9.2 95.7 all-gather.1
  113.6 290.8 all-reduce.1
  406.9 143.5 reduce-scatter.2
  625.2 115.1 reduce-scatter.4
where the time goes:
time: 751 us
  matrix products  345 us (46%)
  waiting for transfers between devices  257 us (34%)
  blocking collectives  96 us (13%)
  other arithmetic  34.5 us (5%)
  between operations  13.2 us (2%)
    dot_general x1, matrix products, per_device(): lax.dot_general(column_rows, lower_tile, (((0,), (1,)), ((), ())), precis...  221 us
    dot_general x1, matrix products, per_device(): lax.dot_general(lower_tile, row_band, (((0,), (0,)), ((), ())), precision...  124 us
    reduce_scatter x1, waiting for transfers between devices, per_device(): lax.psum_scatter(lax.dot_general(column_rows, lower_tile, (((0,), (1,)),...  115 us
    all_to_all x1, blocking collectives, per_device(): lax.all_to_all(upper_part, ('col', 'rep'), split_axis=1, concat_axis=0, t...  96 us
    all_gather x1, waiting for transfers between devices, per_device(): row_band = lax.all_gather(input_panel, ('col', 'rep'), axis=1, tiled=True)  74 us
    psum x1, waiting for transfers between devices, from_root(): return lax.psum(jnp.where(mine, x, jnp.zeros_like(x)), axis)  66.9 us
    dot_general x1, other arithmetic, per_device(): lax.dot_general(lower_tile, row_band, (((0,), (0,)), ((), ())), precision...  23.6 us
  transfers between devices with their start and end apart: 4, of which 3 were waited for; matrix products, arithmetic and copies ran while one was open for 50% of the time, Pallas kernels for 0%

commit v1 on v0

v1 whole, which is shorter than its diff:
```python
import jax
import jax.numpy as jnp
from jax import lax
from jax.sharding import PartitionSpec as P

GROUP = ("col", "rep")


def product(left, right, contract):
    return lax.dot_general(
        left,
        right,
        (contract, ((), ())),
        precision=lax.Precision.HIGH,
        preferred_element_type=jnp.float32,
    )


def after(value, *first):
    return lax.optimization_barrier((value,) + first)[0]


def rows_up(own, rows):
    me = lax.axis_index("row")
    gathered = jnp.zeros((rows,) + own.shape, own.dtype)
    held = early = own
    for step in range(rows):
        slot = lax.rem(me + rows - step, rows)
        gathered = lax.dynamic_update_slice_in_dim(gathered, held[None], slot, 0)
        if step < rows - 1:
            held = lax.ppermute(held, "row", [(r, r + 1) for r in range(step, rows - 1)])
            if step < rows - 2:
                early = held
    return gathered, early


def rows_down(parts, rows):
    me = lax.axis_index("row")
    arrived = None
    for step in range(1, rows):
        block = jnp.maximum(me + step - rows, 0)
        term = lax.dynamic_index_in_dim(parts, block, 0, keepdims=False)
        total = term if arrived is None else term + arrived
        arrived = lax.ppermute(total, "row", [(r, r - 1) for r in range(rows - step, rows)])
        if step == 1:
            first = arrived
    own = lax.dynamic_index_in_dim(parts, me, 0, keepdims=False)
    if arrived is None:
        return own, own
    return own + arrived, first


def per_device(rows, groups, upstream, input_panel):
    row_count, col_count = upstream.shape
    width = input_panel.shape[1]
    ratio = row_count // col_count
    row_index = lax.axis_index("row")
    col_index = lax.axis_index(GROUP)
    rows_global = row_index * row_count + lax.broadcasted_iota(jnp.int32, (row_count, col_count), 0)
    cols_global = col_index * col_count + lax.broadcasted_iota(jnp.int32, (row_count, col_count), 1)
    lower_tile = jnp.where(cols_global <= rows_global, upstream, jnp.float32(0.0))

    panel_t = jnp.transpose(input_panel)
    band_t = lax.all_gather(panel_t, GROUP, axis=0, tiled=True)
    pieces = jnp.transpose(input_panel.reshape(ratio, col_count, width), (0, 2, 1))
    column_blocks, early = rows_up(pieces, rows)
    column_blocks = column_blocks.reshape(groups, width, col_count)

    upper_t = product(after(band_t, early), lower_tile, ((1,), (0,)))
    upper_blocks = lax.all_to_all(
        upper_t.reshape(groups, width, col_count), GROUP, split_axis=0, concat_axis=0, tiled=True
    )
    upper_total, first = rows_down(upper_blocks.reshape(rows, ratio, width, col_count), rows)

    column_t = lax.all_to_all(
        after(column_blocks, upper_blocks), GROUP, split_axis=0, concat_axis=0, tiled=True
    )
    lower_t = product(after(column_t, first).reshape(groups * width, col_count), lower_tile, ((1,), (1,)))
    lower_total = lax.psum_scatter(lower_t, GROUP, scatter_dimension=0, tiled=True)

    upper_rows = jnp.transpose(upper_total, (0, 2, 1)).reshape(row_count, width)
    return upper_rows + jnp.transpose(lower_total)


def solution(mesh):
    rows = mesh.shape["row"]
    groups = mesh.shape["col"] * mesh.shape["rep"]
    placed = P("row", GROUP)

    def body(upstream, input_panel):
        return per_device(rows, groups, upstream, input_panel)

    return jax.shard_map(
        body, mesh=mesh, in_specs=(placed, placed), out_specs=placed, check_vma=False
    )
```

time: 751 us -> 559 us (0.74)
  matrix products: 345 us -> 124 us
  blocking collectives: 96 us -> 0 us
  waiting for transfers between devices: 257 us -> 353 us
  starting transfers between devices: 0.13 us -> 24.5 us
  local copies, waits for them, and re-layouts: 5.61 us -> 29.7 us
  other arithmetic: 34.5 us -> 13.6 us
    dot_general x2, matrix products: 345 us -> 124 us  [product(): lax.dot_general(left, right, (contract, ((), ())), precision=lax.Precisio...]
    all_to_all x0 -> x2, waiting for transfers between devices: none -> 159 us  [the longest x1 83.1 us: per_device(): lax.all_to_all(after(column_blocks, upper_blocks), GROUP, split_axis=0, c...]
    ppermute x0 -> x6, waiting for transfers between devices: none -> 143 us  [the longest x3 99.5 us: rows_down(): lax.ppermute(total, 'row', [(r, r - 1) for r in range(rows - step, rows)])]
    reduce_scatter x2 -> x1, waiting for transfers between devices: 115 us -> 6.38 us  [per_device(): lax.psum_scatter(lower_t, GROUP, scatter_dimension=0, tiled=True)]
    all_to_all x1 -> x0, blocking collectives: 96 us -> none  [per_device(): lax.all_to_all(upper_part, ('col', 'rep'), split_axis=1, concat_axis=0, t...]
    psum x1 -> x0, waiting for transfers between devices: 66.9 us -> none  [from_root(): return lax.psum(jnp.where(mine, x, jnp.zeros_like(x)), axis)]
    all_gather x1, waiting for transfers between devices: 74 us -> 43.9 us  [per_device(): band_t = lax.all_gather(panel_t, GROUP, axis=0, tiled=True)]
    dot_general x1 -> x0, other arithmetic: 23.6 us -> none  [per_device(): lax.dot_general(lower_tile, row_band, (((0,), (0,)), ((), ())), precision...]
  transfers between devices with their start and end apart: 4 -> 10, of which waited for: 3 -> 6; matrix products, arithmetic and copies ran while one was open for 50% -> 7% of each run, Pallas kernels for 0% -> 0%
where the time goes in v1:
time: 559 us
  waiting for transfers between devices  353 us (63%)
  matrix products  124 us (22%)
  local copies, waits for them, and re-layouts  29.7 us (5%)
  starting transfers between devices  24.5 us (4%)
  other arithmetic  13.6 us (2%)
  between operations  13.5 us (2%)
    dot_general x2, matrix products, product(): lax.dot_general(left, right, (contract, ((), ())), precision=lax.Precisio...  124 us
    ppermute x3, waiting for transfers between devices, rows_down(): lax.ppermute(total, 'row', [(r, r - 1) for r in range(rows - step, rows)])  99.5 us
    all_to_all x1, waiting for transfers between devices, per_device(): lax.all_to_all(after(column_blocks, upper_blocks), GROUP, split_axis=0, c...  83.1 us
    all_to_all x1, waiting for transfers between devices, per_device(): lax.all_to_all(upper_t.reshape(groups, width, col_count), GROUP, split_ax...  76.3 us
    all_gather x1, waiting for transfers between devices, per_device(): band_t = lax.all_gather(panel_t, GROUP, axis=0, tiled=True)  43.9 us
    ppermute x3, waiting for transfers between devices, rows_up(): lax.ppermute(held, 'row', [(r, r + 1) for r in range(step, rows - 1)])  43.5 us
  transfers between devices with their start and end apart: 10, of which 6 were waited for; matrix products, arithmetic and copies ran while one was open for 7% of the time, Pallas kernels for 0%

profile of v1, /device:TPU:0, one launch (start us, length us, event | category | flops | bytes accessed | tf_op | source)
XLA Modules:
  0.0 558.5 jit_solution(15312995943313500061)
XLA Ops:
  6.5 0.0 all-gather.2.cloned.1.call-start
  6.5 0.7 all-gather.2.cloned.1.call-update
  7.3 1.9 copy.8
  9.2 6.3 %collective-permute-start = (f32[2,128,2048]{2,1,0:T(8,128)S(1)}, f32[2,128,2048]{2,1,0:T(8,128)}, u32[]{:S(2)}, u32[]{:S(2)}) collective-permute-start(f32[2,128,2048]{2,1,0:T(8,128)S(1)} %bitcast.41), channel_id=1, source_target_pairs={{0,8},{8,16},{16,24},{1,9},{9,17},{17,25},{2,10},{10,18},{18,26},{... | collective-permute-start | bytes 6291464 | tf_op jit(solution)/shard_map/ppermute | solution.py:31
  15.5 43.5 %collective-permute-done = f32[2,128,2048]{2,1,0:T(8,128)} collective-permute-done((f32[2,128,2048]{2,1,0:T(8,128)S(1)}, f32[2,128,2048]{2,1,0:T(8,128)}, u32[]{:S(2)}, u32[]{:S(2)}) %collective-permute-start) | collective-permute-done | bytes 2097184 | tf_op jit(solution)/shard_map/ppermute | solution.py:31
  59.0 2.0 collective-permute-start.1
  61.1 0.0 collective-permute-done.1
  61.1 43.9 %all-gather.2.cloned.1.call-done = f32[1024,4096]{0,1:T(8,128)} async-done(((f32[128,4096]{0,1:T(8,128)}), f32[1024,4096]{0,1:T(8,128)}) %all-gather.2.cloned.1.call-update) | async-done | bytes 16777232 | tf_op jit(solution)/shard_map/all_gather | solution.py:64
  105.0 62.6 %fusion.1 = f32[1024,2048]{1,0:T(8,128)} fusion(f32[1024,4096]{0,1:T(8,128)} %all-gather.2.cloned.1.call-done, f32[4096,2048]{1,0:T(8,128)} %param.2, s32[2048]{0:T(1024)S(1)} %iota_add_fusion.1, s32[4096]{0:T(1024)S(1)} %iota_add_fusion), kind=kOutput, calls=%fused_computation.2 | convolution fusion | flops 51556384768 | bytes 58744832 | tf_op jit(solution)/shard_map/dot_general | solution.py:10
  167.6 5.0 all-to-all-start
  172.6 2.0 collective-permute-start.5
  174.6 4.3 broadcast_in_dim.20
  178.9 1.5 bitcast_dynamic-update-slice_fusion
  180.4 3.1 bitcast_dynamic-update-slice_fusion.3
  183.5 3.1 bitcast_dynamic-update-slice_fusion.2
  186.7 0.0 collective-permute-done.5
  186.7 3.1 bitcast_dynamic-update-slice_fusion.1
  189.8 76.3 %all-to-all-done = f32[8,128,2048]{2,1,0:T(8,128)} async-done(((f32[8,128,2048]{2,1,0:T(8,128)}), f32[8,128,2048]{2,1,0:T(8,128)}, u32[]{:S(2)}, u32[]{:S(2)}) %all-to-all-start) | async-done | bytes 8388640 | tf_op jit(solution)/shard_map/all_to_all | solution.py:70
  266.1 5.0 all-to-all-start.1
  271.0 0.2 reduce-scatter.2.cloned.1.call-start
  271.3 6.5 %constant_dynamic-slice_fusion.3 = (f32[1,2,128,2048]{3,2,1,0:T(8,128)S(1)}, f32[1,2,128,2048]{3,2,1,0:T(8,128)S(1)}, f32[1,2,128,2048]{3,2,1,0:T(8,128)}, f32[1,2,128,2048]{3,2,1,0:T(8,128)}) fusion(f32[4,2,128,2048]{3,2,1,0:T(8,128)} %bitcast.4, s32[]{:T(128)S(6)} %select_n.24, s32[]{:T(128)S(6)} %max.11, s32[]{:T(128)S(6)} %max.10, s32[]{:T(128)S(6)} %max.9), kind=kLoop, calls=%fused_computation.23 | loop fusion | bytes 16777232 | tf_op jit(solution)/shard_map/jit(dynamic_index_in_dim)/dynamic_slice | solution.py:47
  277.7 1.6 copy.19
  279.4 2.0 collective-permute-start.2
  281.4 0.0 collective-permute-done.2
  281.4 83.1 %all-to-all-done.1 = f32[8,128,2048]{2,1,0:T(8,128)} async-done(((f32[8,128,2048]{2,1,0:T(8,128)}), f32[8,128,2048]{2,1,0:T(8,128)}, u32[]{:S(2)}, u32[]{:S(2)}) %all-to-all-start.1) | async-done | bytes 8388640 | tf_op jit(solution)/shard_map/all_to_all | solution.py:75
  364.5 61.1 %fusion = f32[1024,4096]{1,0:T(8,128)} fusion(f32[1024,2048]{1,0:T(8,128)} %bitcast.15, f32[4096,2048]{1,0:T(8,128)} %param.2, s32[2048]{0:T(1024)S(1)} %iota_add_fusion.1, s32[4096]{0:T(1024)S(1)} %iota_add_fusion), kind=kOutput, calls=%fused_computation.1 | convolution fusion | flops 51556384768 | bytes 58744832 | tf_op jit(solution)/shard_map/dot_general | solution.py:10
  425.6 0.0 reduce-scatter.2.cloned.1.call-update
  425.6 4.4 bitcast_add_fusion.1
  430.0 0.8 collective-permute-start.3
  430.8 0.0 collective-permute-done.3
  430.8 3.8 bitcast_add_fusion.2
  434.6 1.3 collective-permute-start.4
  435.9 99.5 %collective-permute-done.4 = f32[2,128,2048]{2,0,1:T(2,128)S(1)} collective-permute-done((f32[2,128,2048]{2,0,1:T(2,128)S(1)}, f32[2,128,2048]{2,0,1:T(2,128)S(1)}, u32[]{:S(2)}, u32[]{:S(2)}) %collective-permute-start.4) | collective-permute-done | bytes 2097184 | tf_op jit(solution)/shard_map/ppermute | solution.py:44
  535.4 2.2 bitcast_add_fusion.3
  537.6 1.6 copy.14
  539.3 6.4 %reduce-scatter.2.cloned.1.call-done = f32[128,4096]{1,0:T(8,128)} async-done(((f32[1024,4096]{1,0:T(8,128)}), f32[128,4096]{1,0:T(8,128)}) %reduce-scatter.2.cloned.1.call-update) | async-done | bytes 2097168 | tf_op jit(solution)/shard_map/reduce_scatter | solution.py:79
  545.6 3.2 bitcast_add_fusion
  548.8 2.9 copy.13
  (2 shorter events, 0.0 us)
Async XLA Ops:
  6.5 98.5 %all-gather.2.cloned.1.call-start = ((), (), s32[]{:S(2)}) async-start(), calls=%async_computation.3 | async-start | bytes 18874368 | tf_op jit(solution)/shard_map/all_gather | solution.py:64
  9.2 49.8 %collective-permute-start = (f32[2,128,2048]{2,1,0:T(8,128)S(1)}, f32[2,128,2048]{2,1,0:T(8,128)}, u32[]{:S(2)}, u32[]{:S(2)}) collective-permute-start(f32[2,128,2048]{2,1,0:T(8,128)S(1)} %bitcast.41), channel_id=1, source_target_pairs={{0,8},{8,16},{16,24},{1,9},{9,17},{17,25},{2,10},{10,18},{18,26},{... | collective-permute-start | bytes 6291464 | tf_op jit(solution)/shard_map/ppermute | solution.py:31
  59.0 2.0 collective-permute-start.1
  167.6 98.4 %all-to-all-start = ((f32[8,128,2048]{2,1,0:T(8,128)}), f32[8,128,2048]{2,1,0:T(8,128)}, u32[]{:S(2)}, u32[]{:S(2)}) async-start(f32[8,128,2048]{2,1,0:T(8,128)} %bitcast.38), calls=%async_computation | async-start | bytes 16777216 | tf_op jit(solution)/shard_map/all_to_all | solution.py:70
  172.6 14.1 %collective-permute-start.5 = (f32[2,128,2048]{2,1,0:T(8,128)}, f32[2,128,2048]{2,1,0:T(8,128)}, u32[]{:S(2)}, u32[]{:S(2)}) collective-permute-start(f32[2,128,2048]{2,1,0:T(8,128)} %collective-permute-done.1), channel_id=1, source_target_pairs={{16,24},{17,25},{18,26},{19,27},{20,28},{21,29},{22,30},{23,31}} | collective-permute-start | bytes 6291464 | tf_op jit(solution)/shard_map/ppermute | solution.py:31
  266.1 98.4 %all-to-all-start.1 = ((f32[8,128,2048]{2,1,0:T(8,128)}), f32[8,128,2048]{2,1,0:T(8,128)}, u32[]{:S(2)}, u32[]{:S(2)}) async-start(f32[8,128,2048]{2,1,0:T(8,128)} %bitcast.14), calls=%async_computation.1 | async-start | bytes 16777216 | tf_op jit(solution)/shard_map/all_to_all | solution.py:75
  271.0 274.6 %reduce-scatter.2.cloned.1.call-start = ((), (), s32[]{:S(2)}) async-start(), calls=%async_computation.4 | async-start | bytes 18874368 | tf_op jit(solution)/shard_map/reduce_scatter | solution.py:79
  279.4 2.0 collective-permute-start.2
  430.0 0.8 collective-permute-start.3
  434.6 100.8 %collective-permute-start.4 = (f32[2,128,2048]{2,0,1:T(2,128)S(1)}, f32[2,128,2048]{2,0,1:T(2,128)S(1)}, u32[]{:S(2)}, u32[]{:S(2)}) collective-permute-start(f32[2,128,2048]{2,0,1:T(2,128)S(1)} %bitcast_add_fusion.2), channel_id=1, source_target_pairs={{8,0},{16,8},{24,16},{9,1},{17,9},{25,17},{10,2},{18,10},{26,18},{... | collective-permute-start | bytes 6291464 | tf_op jit(solution)/shard_map/ppermute | solution.py:44
Sparse Core Ops, SparseCore 0:
  9.2 95.7 all-gather.1
  425.7 119.8 reduce-scatter.1
